TPU v7x, 32 devices: a whole 2x2x4 slice. The times are simulated.
32 devices in a mesh: dp: 8 (over z, y), tensor: 4 (over x, core).
Axes of the slice: x: 2, y: 2, z: 4, core: 2. Of those that a mesh axis runs over, the one named last changes fastest.
Arguments:
- logits: bfloat16 [32, 64, 152064], P('dp', None, 'tensor'), may hold values from -3 to 3
- tokens: int32 [32, 64], P('dp'), may hold values from 0 to 152063
- lengths: int32 [32], P('dp'), may hold values from 1 to 64, 1024 in all
- group_ids: int32 [32], P('dp'), may hold values from 0 to 1, as said below
- rewards: float32 [32], P('dp'), may hold values from -4 to 4
- old_logp: float32 [32, 64], P('dp'), may hold values from -12.6 to -11.5
- ref_logp: float32 [32, 64], P('dp'), may hold values from -12.6 to -11.5
Outputs:
- token_logp: float32 [32, 64], P('dp')
- advantages: float32 [32], P('dp')
- seq_loss: float32 [32], P('dp')
- total_loss: float32 [], replicated
Inputs may be any that keep to these rules, and one draw needn't show every extreme that they name: `group_ids`: each number 0 to 1 names exactly 16 responses, placed at random over the batch. `lengths`: each response has 1 to 64 tokens, the longest exactly 64.
All inputs are finite; a program needn't handle non-finite values.
Results may differ from a plain program's by a relative error of at most 0.0003.
Values sent between devices are 32-bit elements.
A program may use at most 128 MiB of HBM per device.

v0:
```python
import jax
import jax.numpy as jnp
from jax import lax
from jax.sharding import PartitionSpec as P

GROUP = 16
CLIP_LOW = 0.2
CLIP_HIGH = 0.28
KL_WEIGHT = 0.04
STD_EPS = 0.0001


def combined_all(value, axis, join):
    pieces = jax.tree.map(lambda part: lax.all_gather(part, axis), value)
    head = jax.tree.map(lambda part: part[0], pieces)
    tail = jax.tree.map(lambda part: part[1:], pieces)
    total, _ = lax.scan(lambda total, slab: (join(total, slab), None), head, tail)
    return total


def combine_pair(former, latter):
    row_peak = jnp.maximum(former[0], latter[0])
    row_total = former[1] * jnp.exp(former[0] - row_peak) + latter[1] * jnp.exp(
        latter[0] - row_peak
    )
    return (row_peak, row_total)


def block_stats(logit_block, local_ids, vocab_width):
    values = logit_block.astype(jnp.float32)
    row_peak = jnp.max(values, axis=-1)
    row_total = jnp.sum(jnp.exp(values - row_peak[..., None]), axis=-1)
    inside = (local_ids >= 0) & (local_ids < vocab_width)
    clamped = jnp.clip(local_ids, 0, vocab_width - 1)
    picked = jnp.take_along_axis(values, clamped[..., None], axis=-1)[..., 0]
    return (row_peak, row_total, jnp.where(inside, picked, 0.0))


def local(logits, tokens, lengths, group_ids, rewards, old_logp, ref_logp):
    resp_count, seq_len, vocab_width = logits.shape
    vocab_start = lax.axis_index("tensor") * vocab_width
    local_ids = tokens - vocab_start
    positions = lax.broadcasted_iota(jnp.int32, (resp_count, seq_len), 1)
    is_valid = positions < lengths[:, None]
    row_peak, row_total, picked = block_stats(logits, local_ids, vocab_width)
    row_peak, row_total = combined_all((row_peak, row_total), "tensor", combine_pair)
    picked = lax.psum(picked, "tensor")
    token_logp = jnp.where(is_valid, picked - row_peak - jnp.log(row_total), 0.0)
    group_count = resp_count * lax.axis_size("dp") // GROUP
    group_sum, squares = lax.psum(
        (
            jax.ops.segment_sum(rewards, group_ids, num_segments=group_count),
            jax.ops.segment_sum(rewards * rewards, group_ids, num_segments=group_count),
        ),
        "dp",
    )
    group_mean = group_sum / GROUP
    spread = rewards - group_mean[group_ids]
    deviation = jnp.sqrt(jnp.maximum(squares - group_sum * group_mean, 0.0) / (GROUP - 1))
    advantages = spread / (deviation[group_ids] + STD_EPS)
    prob_ratio = jnp.exp(token_logp - old_logp)
    clipped = jnp.clip(prob_ratio, 1.0 - CLIP_LOW, 1.0 + CLIP_HIGH)
    token_gain = advantages[:, None]
    policy = -jnp.minimum(prob_ratio * token_gain, clipped * token_gain)
    ref_drift = ref_logp - token_logp
    penalty = jnp.exp(ref_drift) - ref_drift - 1.0
    token_terms = jnp.where(is_valid, policy + KL_WEIGHT * penalty, 0.0)
    seq_loss = jnp.sum(token_terms, axis=1) / lengths.astype(jnp.float32)
    total_loss = lax.psum(jnp.sum(seq_loss), "dp") / (resp_count * lax.axis_size("dp"))
    return (token_logp, advantages, seq_loss, total_loss)


def solution(mesh):
    in_specs = (
        P("dp", None, "tensor"),
        P("dp", None),
        P("dp"),
        P("dp"),
        P("dp"),
        P("dp", None),
        P("dp", None),
    )
    out_specs = (P("dp", None), P("dp"), P("dp"), P())
    return jax.shard_map(local, mesh=mesh, in_specs=in_specs, out_specs=out_specs, check_vma=False)
```

profile of v0, /device:TPU:0, one launch (start us, length us, event | category | flops | bytes accessed | tf_op | source)
XLA Modules:
  0.0 109.3 jit_solution(2576854799696201980)
XLA Ops:
  0.6 0.0 copy-start
  0.6 0.7 compare_select_fusion.1
  1.3 0.7 scatter_custom_fusion
  2.0 0.7 mul.36
  2.8 0.7 scatter_custom_fusion.1
  3.5 23.2 %all-reduce = (f32[2]{0:T(128)S(1)}, f32[2]{0:T(128)S(1)}) all-reduce(f32[2]{0:T(128)S(1)} %scatter_custom_fusion.1, f32[2]{0:T(128)S(1)} %scatter_custom_fusion), channel_id=1, replica_groups=mesh['dp'=8,'tensor'=4] {'dp'}, use_global_device_ids=true, to_apply=%region_8.9 | all-reduce | flops 4 | bytes 32 | tf_op jit(solution)/shard_map/psum | solution.py:50
  26.7 0.7 fusion.12
  27.4 0.1 reshape.64
  27.5 0.6 gather_fusion.1
  28.1 0.6 gather_fusion
  28.8 0.7 add_divide_fusion
  29.4 0.0 copy-start.4
  29.4 28.6 %fusion.18 = (f32[4,64,38016]{2,1,0:T(8,128)}, bf16[4,64]{1,0:T(4,128)(2,1)S(1)}) fusion(bf16[4,64,38016]{2,1,0:T(8,128)(2,1)} %param.9), kind=kLoop, calls=%fused_computation.45 | loop fusion | flops 19463936 | bytes 58393088 | tf_op jit(solution)/shard_map/convert_element_type | solution.py:30
  58.0 4.2 %gather_fusion.2 = f32[256]{0:T(256)S(1)} fusion(f32[4,64,38016]{2,1,0:T(8,128)} %get-tuple-element.52, s32[256]{0:T(256)S(1)} %reshape.64), kind=kCustom, calls=%fused_computation.2 | custom fusion | bytes 5120 | tf_op jit(solution)/shard_map/jit(take_along_axis)/gather | solution.py:35
  62.2 0.1 gather.13
  62.3 0.0 copy-done
  62.3 5.7 %psum.28 = f32[4,64]{1,0:T(4,128)S(1)} all-reduce(f32[4,64]{1,0:T(4,128)S(1)} %select_select_fusion), channel_id=1, replica_groups=mesh['dp'=8,'tensor'=4] {'tensor'}, use_global_device_ids=true, to_apply=%region_0.0 | all-reduce | flops 256 | bytes 2048 | tf_op jit(solution)/shard_map/psum | solution.py:47
  68.0 9.4 %exponential_reduce_fusion = f32[4,64]{1,0:T(4,128)S(1)} fusion(f32[4,64]{1,0:T(4,128)S(1)} %get-tuple-element.54, bf16[4,64,38016]{2,1,0:T(8,128)(2,1)} %param.9), kind=kLoop, calls=%fused_computation.10 | loop fusion | flops 29196032 | bytes 19466240 | tf_op jit(solution)/shard_map/reduce_sum | solution.py:32
  77.4 5.2 %all-gather.3 = f32[4,4,64]{2,1,0:T(4,128)S(1)} all-gather(f32[1,4,64]{2,1,0:T(4,128)S(1)} %bitcast.27), channel_id=3, replica_groups=mesh['dp'=8,'tensor'=4] {'tensor'}, dimensions={0}, use_global_device_ids=true | all-gather | bytes 5120 | tf_op jit(solution)/shard_map/all_gather | solution.py:14
  82.6 5.2 %all-gather.2 = f32[4,4,64]{2,1,0:T(4,128)S(1)} all-gather(f32[1,4,64]{2,1,0:T(4,128)S(1)} %get-tuple-element.55), channel_id=2, replica_groups=mesh['dp'=8,'tensor'=4] {'tensor'}, dimensions={0}, use_global_device_ids=true | all-gather | bytes 5120 | tf_op jit(solution)/shard_map/all_gather | solution.py:14
  87.8 0.1 while.12
  87.9 0.8 fusion.11
  88.7 1.1 %fusion.17 = (f32[]{:T(128)}, f32[4]{0:T(128)}) fusion(f32[4]{0:T(128)S(1)} %get-tuple-element.50, s32[4]{0:T(128)S(1)} %copy-done.1), kind=kLoop, calls=%fused_computation.44 | loop fusion | flops 11 | bytes 52 | tf_op jit(solution)/shard_map/reduce_sum | solution.py:69
  89.8 17.7 %psum.31 = f32[]{:T(128)} all-reduce(f32[]{:T(128)} %get-tuple-element.48), channel_id=1, replica_groups=mesh['dp'=8,'tensor'=4] {'dp'}, use_global_device_ids=true, to_apply=%region_11.12 | all-reduce | flops 1 | bytes 8 | tf_op jit(solution)/shard_map/psum | solution.py:69
  (22 shorter events, 0.1 us)
Async XLA Ops:
  0.6 61.7 %copy-start = (s32[4,64]{1,0:T(4,128)S(1)}, s32[4,64]{1,0:T(4,128)}, u32[]{:S(2)}) copy-start(s32[4,64]{1,0:T(4,128)} %param.10) | copy-start | bytes 3076
  29.4 58.5 %copy-start.2 = (f32[4]{0:T(128)}, f32[4]{0:T(128)S(1)}, u32[]{:S(2)}) copy-start(f32[4]{0:T(128)S(1)} %add_divide_fusion) | copy-start | bytes 52
  29.4 58.5 %copy-start.1 = (s32[4]{0:T(128)S(1)}, s32[4]{0:T(128)}, u32[]{:S(2)}) copy-start(s32[4]{0:T(128)} %param.11) | copy-start | bytes 52
  29.4 58.5 %copy-start.3 = (f32[4,64]{1,0:T(4,128)S(1)}, f32[4,64]{1,0:T(4,128)}, u32[]{:S(2)}) copy-start(f32[4,64]{1,0:T(4,128)} %param.15) | copy-start | bytes 3076
  29.4 58.5 %copy-start.4 = (f32[4,64]{1,0:T(4,128)S(1)}, f32[4,64]{1,0:T(4,128)}, u32[]{:S(2)}) copy-start(f32[4,64]{1,0:T(4,128)} %param.14) | copy-start | bytes 3076
where the time goes:
time: 110 us; the launch traced here: 109 us
  blocking collectives  56.9 us (52%)
  other arithmetic  44.2 us (40%)
  local copies, waits for them, and re-layouts  5.64 us (5%)
  between operations  2.52 us (2%)
    convert_element_type x1, other arithmetic, block_stats(): values = logit_block.astype(jnp.float32)  28.6 us
    psum x1, blocking collectives, local(): lax.psum((jax.ops.segment_sum(rewards, group_ids, num_segments=group_coun...  23.2 us
    psum x1, blocking collectives, local(): lax.psum(jnp.sum(seq_loss), 'dp') / (resp_count * lax.axis_size('dp'))  17.7 us
    all_gather x2, blocking collectives, combined_all(): pieces = jax.tree.map(lambda part: lax.all_gather(part, axis), value)  10.4 us
    reduce_sum x1, other arithmetic, block_stats(): row_total = jnp.sum(jnp.exp(values - row_peak[..., None]), axis=-1)  9.42 us
    psum x1, blocking collectives, local(): picked = lax.psum(picked, 'tensor')  5.67 us
    gather x3, local copies, waits for them, and re-layouts, block_stats(): picked = jnp.take_along_axis(values, clamped[..., None], axis=-1)[..., 0]  4.33 us

commit v1 on v0

--- a/solution.py
+++ b/solution.py
@@ -44,7 +44,7 @@
     is_valid = positions < lengths[:, None]
     row_peak, row_total, picked = block_stats(logits, local_ids, vocab_width)
     row_peak, row_total = combined_all((row_peak, row_total), "tensor", combine_pair)
-    picked = lax.psum(picked, "tensor")
+    picked = jnp.sum(lax.all_gather(picked, "tensor"), axis=0)
     token_logp = jnp.where(is_valid, picked - row_peak - jnp.log(row_total), 0.0)
     group_count = resp_count * lax.axis_size("dp") // GROUP
     group_sum, squares = lax.psum(

time: 110 us -> 109 us (level)
    psum x1 -> x0, blocking collectives: 5.67 us -> none  [local(): picked = lax.psum(picked, 'tensor')]
    all_gather x0 -> x1, blocking collectives: none -> 5.18 us  [local(): picked = jnp.sum(lax.all_gather(picked, 'tensor'), axis=0)]
where the time goes in v1:
time: 109 us
  blocking collectives  56.4 us (52%)
  other arithmetic  44.2 us (41%)
  local copies, waits for them, and re-layouts  5.64 us (5%)
  between operations  2.53 us (2%)
    convert_element_type x1, other arithmetic, block_stats(): values = logit_block.astype(jnp.float32)  28.6 us
    psum x1, blocking collectives, local(): lax.psum((jax.ops.segment_sum(rewards, group_ids, num_segments=group_coun...  23.2 us
    psum x1, blocking collectives, local(): lax.psum(jnp.sum(seq_loss), 'dp') / (resp_count * lax.axis_size('dp'))  17.7 us
    all_gather x2, blocking collectives, combined_all(): pieces = jax.tree.map(lambda part: lax.all_gather(part, axis), value)  10.4 us
    reduce_sum x1, other arithmetic, block_stats(): row_total = jnp.sum(jnp.exp(values - row_peak[..., None]), axis=-1)  9.43 us
    all_gather x1, blocking collectives, local(): picked = jnp.sum(lax.all_gather(picked, 'tensor'), axis=0)  5.18 us
    gather x3, local copies, waits for them, and re-layouts, block_stats(): picked = jnp.take_along_axis(values, clamped[..., None], axis=-1)[..., 0]  4.33 us

profile of v1, /device:TPU:0, one launch (start us, length us, event | category | flops | bytes accessed | tf_op | source)
XLA Modules:
  0.0 108.9 jit_solution(844881406953367981)
XLA Ops:
  0.6 0.0 copy-start
  0.6 0.7 compare_select_fusion.1
  1.3 0.7 scatter_custom_fusion
  2.0 0.7 mul.36
  2.8 0.7 scatter_custom_fusion.1
  3.5 23.2 %all-reduce = (f32[2]{0:T(128)S(1)}, f32[2]{0:T(128)S(1)}) all-reduce(f32[2]{0:T(128)S(1)} %scatter_custom_fusion.1, f32[2]{0:T(128)S(1)} %scatter_custom_fusion), channel_id=1, replica_groups=mesh['dp'=8,'tensor'=4] {'dp'}, use_global_device_ids=true, to_apply=%region_8.9 | all-reduce | flops 4 | bytes 32 | tf_op jit(solution)/shard_map/psum | solution.py:50
  26.7 0.7 fusion.12
  27.4 0.1 reshape.64
  27.5 0.6 gather_fusion.1
  28.1 0.6 gather_fusion
  28.8 0.7 add_divide_fusion
  29.4 0.0 copy-start.4
  29.4 28.6 %fusion.18 = (f32[4,64,38016]{2,1,0:T(8,128)}, bf16[4,64]{1,0:T(4,128)(2,1)S(1)}) fusion(bf16[4,64,38016]{2,1,0:T(8,128)(2,1)} %param.9), kind=kLoop, calls=%fused_computation.45 | loop fusion | flops 19463936 | bytes 58393088 | tf_op jit(solution)/shard_map/convert_element_type | solution.py:30
  58.0 4.2 %gather_fusion.2 = f32[256]{0:T(256)S(1)} fusion(f32[4,64,38016]{2,1,0:T(8,128)} %get-tuple-element.52, s32[256]{0:T(256)S(1)} %reshape.64), kind=kCustom, calls=%fused_computation.2 | custom fusion | bytes 5120 | tf_op jit(solution)/shard_map/jit(take_along_axis)/gather | solution.py:35
  62.2 0.1 gather.13
  62.3 0.0 copy-done
  62.3 9.4 %exponential_reduce_fusion = f32[4,64]{1,0:T(4,128)S(1)} fusion(f32[4,64]{1,0:T(4,128)S(1)} %get-tuple-element.54, bf16[4,64,38016]{2,1,0:T(8,128)(2,1)} %param.9), kind=kLoop, calls=%fused_computation.10 | loop fusion | flops 29196032 | bytes 19466240 | tf_op jit(solution)/shard_map/reduce_sum | solution.py:32
  71.7 5.2 %all-gather.5 = f32[4,4,64]{2,1,0:T(4,128)S(1)} all-gather(f32[1,4,64]{2,1,0:T(4,128)S(1)} %bitcast.29), channel_id=4, replica_groups=mesh['dp'=8,'tensor'=4] {'tensor'}, dimensions={0}, use_global_device_ids=true | all-gather | bytes 5120 | tf_op jit(solution)/shard_map/all_gather | solution.py:14
  76.9 5.2 %all-gather.3 = f32[4,4,64]{2,1,0:T(4,128)S(1)} all-gather(f32[1,4,64]{2,1,0:T(4,128)S(1)} %select_bitcast_fusion), channel_id=2, replica_groups=mesh['dp'=8,'tensor'=4] {'tensor'}, dimensions={0}, use_global_device_ids=true | all-gather | bytes 5120 | tf_op jit(solution)/shard_map/all_gather | solution.py:47
  82.1 5.2 %all-gather.4 = f32[4,4,64]{2,1,0:T(4,128)S(1)} all-gather(f32[1,4,64]{2,1,0:T(4,128)S(1)} %get-tuple-element.55), channel_id=3, replica_groups=mesh['dp'=8,'tensor'=4] {'tensor'}, dimensions={0}, use_global_device_ids=true | all-gather | bytes 5120 | tf_op jit(solution)/shard_map/all_gather | solution.py:14
  87.3 0.1 while.12
  87.4 0.8 fusion.11
  88.2 1.1 %fusion.17 = (f32[]{:T(128)}, f32[4]{0:T(128)}) fusion(f32[4]{0:T(128)S(1)} %get-tuple-element.50, s32[4]{0:T(128)S(1)} %copy-done.1), kind=kLoop, calls=%fused_computation.44 | loop fusion | flops 11 | bytes 52 | tf_op jit(solution)/shard_map/reduce_sum | solution.py:69
  89.3 17.7 %psum.23 = f32[]{:T(128)} all-reduce(f32[]{:T(128)} %get-tuple-element.48), channel_id=1, replica_groups=mesh['dp'=8,'tensor'=4] {'dp'}, use_global_device_ids=true, to_apply=%region_11.12 | all-reduce | flops 1 | bytes 8 | tf_op jit(solution)/shard_map/psum | solution.py:69
  (23 shorter events, 0.2 us)
Async XLA Ops:
  0.6 61.7 %copy-start = (s32[4,64]{1,0:T(4,128)S(1)}, s32[4,64]{1,0:T(4,128)}, u32[]{:S(2)}) copy-start(s32[4,64]{1,0:T(4,128)} %param.10) | copy-start | bytes 3076
  29.4 58.0 %copy-start.2 = (f32[4]{0:T(128)}, f32[4]{0:T(128)S(1)}, u32[]{:S(2)}) copy-start(f32[4]{0:T(128)S(1)} %add_divide_fusion) | copy-start | bytes 52
  29.4 58.0 %copy-start.1 = (s32[4]{0:T(128)S(1)}, s32[4]{0:T(128)}, u32[]{:S(2)}) copy-start(s32[4]{0:T(128)} %param.11) | copy-start | bytes 52
  29.4 58.0 %copy-start.3 = (f32[4,64]{1,0:T(4,128)S(1)}, f32[4,64]{1,0:T(4,128)}, u32[]{:S(2)}) copy-start(f32[4,64]{1,0:T(4,128)} %param.15) | copy-start | bytes 3076
  29.4 58.0 %copy-start.4 = (f32[4,64]{1,0:T(4,128)S(1)}, f32[4,64]{1,0:T(4,128)}, u32[]{:S(2)}) copy-start(f32[4,64]{1,0:T(4,128)} %param.14) | copy-start | bytes 3076
